TPU v7x, 32 devices: a whole 2x2x4 slice. The times are simulated.
32 devices in a mesh: freq: 8 (over y, x, core), feed: 4 (over z).
Axes of the slice: x: 2, y: 2, z: 4, core: 2. Of those that a mesh axis runs over, the one named last changes fastest.
Arguments:
- voltages: int32 [32, 2048, 2, 768], P(None, ('feed', 'freq')), may hold values from -127 to 127
- gains: float32 [2, 32, 2048], P(None, None, ('feed', 'freq')), may hold values from -0.06 to 0.06
Outputs:
- visibilities: float32 [32, 2, 2048, 2048], P('freq', None, 'feed')
All inputs are finite; a program needn't handle non-finite values.
Results may differ from a plain program's by a relative error of at most 0.0031.
Values may be sent and summed in bfloat16 or wider, within the bound.
A program may use at most 192 MiB of HBM per device.

v0:
```python
import jax
import jax.numpy as jnp
from jax import lax
from jax.sharding import PartitionSpec as P


def stack_rows(own_rows, samples):
    real_part = own_rows[..., :samples]
    imag_part = own_rows[..., samples:]
    swapped = jnp.concatenate([imag_part, -real_part], axis=-1)
    return jnp.stack([own_rows, swapped], axis=1)


def correlate(stacked, columns, samples):
    product = jnp.einsum("cqrk,cfk->cqrf", stacked, columns, preferred_element_type=jnp.float32)
    return product * (1.0 / samples)


def per_device(voltages, gains):
    channels = voltages.shape[0]
    local_feeds = voltages.shape[1]
    samples = voltages.shape[3]
    freq_count = lax.axis_size("freq")
    owned = channels // freq_count
    volt_real = voltages[:, :, 0, :].astype(jnp.float32)
    volt_imag = voltages[:, :, 1, :].astype(jnp.float32)
    gain_real = gains[0][:, :, None]
    gain_imag = gains[1][:, :, None]
    eq_real = gain_real * volt_real - gain_imag * volt_imag
    eq_imag = gain_real * volt_imag + gain_imag * volt_real
    equalized = jnp.stack([eq_real, eq_imag], axis=2).astype(jnp.bfloat16)
    blocks = equalized.reshape(freq_count, owned, local_feeds, 2 * samples)
    arrived = lax.all_to_all(blocks, "freq", split_axis=0, concat_axis=2, tiled=True)
    own_rows = arrived[0]
    stacked = stack_rows(own_rows, samples)
    return correlate(stacked, lax.all_gather(own_rows, "feed", axis=1, tiled=True), samples)


def solution(mesh):
    in_specs = (P(None, ("feed", "freq"), None, None), P(None, None, ("feed", "freq")))
    out_specs = P("freq", None, "feed", None)
    return jax.shard_map(
        per_device, mesh=mesh, in_specs=in_specs, out_specs=out_specs, check_vma=False
    )
```

profile of v0, /device:TPU:0, one launch (start us, length us, event | category | flops | bytes accessed | tf_op | source)
XLA Modules:
  0.0 606.3 jit_solution(17884581884118223520)
XLA Ops:
  6.5 0.0 all-gather.2.cloned.1.call-start
  6.5 0.7 slice_bitcast_fusion.1
  7.3 22.8 %subtract_convert_fusion = (bf16[32,64,1,768]{3,2,1,0:T(2,128)(2,1)S(1)}, bf16[32,64,1,768]{3,2,1,0:T(2,128)(2,1)S(1)}) fusion(s32[32,64,2,768]{3,2,1,0:T(2,128)} %param.2, f32[32,64]{1,0:T(8,128)S(1)} %get-tuple-element.10, f32[32,64]{1,0:T(8,128)S(1)} %get-tuple-element.9), kind=kLoop, calls=%fused_computation.8 | loop fusion | flops 15728640 | bytes 18890752 | tf_op jit(solution)/shard_map/convert
  30.0 15.4 %pad_maximum_fusion.1 = bf16[32,64,2,768]{3,2,1,0:T(2,128)(2,1)} fusion(bf16[32,64,1,768]{3,2,1,0:T(2,128)(2,1)S(1)} %get-tuple-element.6, bf16[32,64,1,768]{3,2,1,0:T(2,128)(2,1)S(1)} %get-tuple-element.5), kind=kLoop, calls=%fused_computation.5 | loop fusion | flops 12582912 | bytes 12582912 | tf_op jit(solution)/shard_map/stack | solution.py:31
  45.4 14.4 %convert_element_type.17 = bf16[8,4,64,1536]{3,2,1,0:T(8,128)(2,1)} reshape(bf16[32,64,2,768]{3,2,1,0:T(2,128)(2,1)} %pad_maximum_fusion.1) | data formatting | bytes 12582912 | tf_op jit(solution)/shard_map/convert_element_type | solution.py:31
  59.8 76.7 %all_to_all.15 = bf16[8,4,64,1536]{3,2,1,0:T(8,128)(2,1)S(1)} all-to-all(bf16[8,4,64,1536]{3,2,1,0:T(8,128)(2,1)} %convert_element_type.17), channel_id=1, replica_groups=mesh['freq'=8,'feed'=4] {'freq'}, dimensions={0} | all-to-all | bytes 12582912 | tf_op jit(solution)/shard_map/all_to_all | solution.py:33
  136.5 3.4 copy.5
  139.9 0.0 all-gather.2.cloned.1.call-update
  140.0 3.3 fusion.6
  143.2 3.3 maximum_bitcast_fusion
  146.5 417.1 %all-gather.2.cloned.1.call-done = bf16[4,2048,1536]{2,1,0:T(8,128)(2,1)} async-done(((bf16[4,512,1536]{2,1,0:T(8,128)(2,1)}), bf16[4,2048,1536]{2,1,0:T(8,128)(2,1)}) %all-gather.2.cloned.1.call-update) | async-done | bytes 25165840 | tf_op jit(solution)/shard_map/all_gather | solution.py:36
  563.6 35.8 %fusion.2 = f32[4,2,512,2048]{3,2,1,0:T(8,128)} fusion(bf16[4,2048,1536]{2,1,0:T(8,128)(2,1)} %all-gather.2.cloned.1.call-done, bf16[4,1,512,1536]{3,2,0,1:T(8,128)(2,1)} %maximum_bitcast_fusion, bf16[4,1,512,1536]{3,2,0,1:T(8,128)(2,1)} %bitcast.20), kind=kOutput, calls=%fused_computation.2 | convolution fusion | flops 25784483840 | bytes 71303168 | tf_op jit(solution)/shard_map/cqrk,cfk->cqrf/dot_general | solution.py:15
Async XLA Ops:
  6.5 557.1 %all-gather.2.cloned.1.call-start = ((), (), s32[]{:S(2)}) async-start(), calls=%async_computation.1 | async-start | bytes 31457280 | tf_op jit(solution)/shard_map/all_gather | solution.py:36
Sparse Core Ops, SparseCore 0:
  140.1 423.5 all-gather.1
where the time goes:
time: 607 us; the launch traced here: 606 us
  waiting for transfers between devices  417 us (69%)
  blocking collectives  76.7 us (13%)
  other arithmetic  44.7 us (7%)
  matrix products  35.8 us (6%)
  local copies, waits for them, and re-layouts  18.5 us (3%)
  between operations  13.4 us (2%)
    all_gather x1, waiting for transfers between devices, per_device(): lax.all_gather(own_rows, 'feed', axis=1, tiled=True)  417 us
    all_to_all x1, blocking collectives, per_device(): lax.all_to_all(blocks, 'freq', split_axis=0, concat_axis=2, tiled=True)  76.7 us
    dot_general x1, matrix products, correlate(): jnp.einsum('cqrk,cfk->cqrf', stacked, columns, preferred_element_type=jnp...  35.8 us
    another operation x1, other arithmetic  22.8 us
    another operation x1, other arithmetic, per_device(): equalized = jnp.stack([eq_real, eq_imag], axis=2).astype(jnp.bfloat16)  15.4 us
    convert_element_type x1, local copies, waits for them, and re-layouts, per_device(): equalized = jnp.stack([eq_real, eq_imag], axis=2).astype(jnp.bfloat16)  14.4 us
  transfers between devices with their start and end apart: 1, of which 1 were waited for; matrix products, arithmetic and copies ran while one was open for 1% of the time, Pallas kernels for 0%

commit v1 on v0

v1 whole, which is shorter than its diff:
```python
import jax
import jax.numpy as jnp
from jax import lax
from jax.sharding import PartitionSpec as P

def stack_rows(own_rows, samples):
    real_part = own_rows[..., :samples]
    imag_part = own_rows[..., samples:]
    swapped = jnp.concatenate([imag_part, -real_part], axis=-1)
    return jnp.stack([own_rows, swapped], axis=0)


def correlate(stacked, columns, samples):
    product = jnp.einsum("qrk,fk->qrf", stacked, columns, preferred_element_type=jnp.float32)
    return product * (1.0 / samples)


def ring_blocks(own, count):
    forward = [(source, (source + 1) % count) for source in range(count)]
    backward = [(source, (source - 1) % count) for source in range(count)]
    half = own.shape[0] // 2
    pieces = [(0, 0, own)]
    from_left = from_right = own
    for step in range(1, count):
        if 2 * step > count:
            break
        if 2 * step == count:
            pieces.append((-step, 0, lax.ppermute(from_left[:half], "feed", forward)))
            pieces.append((-step, half, lax.ppermute(from_right[half:], "feed", backward)))
        else:
            from_left = lax.ppermute(from_left, "feed", forward)
            from_right = lax.ppermute(from_right, "feed", backward)
            pieces.append((-step, 0, from_left))
            pieces.append((step, 0, from_right))
    return pieces


def per_device(voltages, gains):
    channels, local_feeds, _, samples = voltages.shape
    freq_count = lax.axis_size("freq")
    feed_count = lax.axis_size("feed")
    position = lax.axis_index("feed")
    owned = channels // freq_count
    rows = local_feeds * freq_count
    volts = voltages.reshape(freq_count, owned, local_feeds, 2, samples)
    scale = gains.reshape(2, freq_count, owned, local_feeds)[..., None]
    visibilities = jnp.zeros((owned, 2, rows, rows * feed_count), jnp.float32)
    for channel in range(owned):
        volt_real = volts[:, channel, :, 0].astype(jnp.float32)
        volt_imag = volts[:, channel, :, 1].astype(jnp.float32)
        gain_real = scale[0, :, channel]
        gain_imag = scale[1, :, channel]
        eq_real = gain_real * volt_real - gain_imag * volt_imag
        eq_imag = gain_real * volt_imag + gain_imag * volt_real
        blocks = jnp.concatenate([eq_real, eq_imag], axis=-1).astype(jnp.bfloat16)
        arrived = lax.all_to_all(blocks, "freq", split_axis=0, concat_axis=0, tiled=True)
        own_rows = arrived.reshape(rows, 2 * samples)
        stacked = stack_rows(own_rows, samples)
        for offset, start, block in ring_blocks(own_rows, feed_count):
            owner = lax.rem(position + offset + feed_count, feed_count)
            visibilities = lax.dynamic_update_slice(
                visibilities,
                correlate(stacked, block, samples)[None],
                (channel, 0, 0, owner * rows + start),
            )
    return visibilities


def solution(mesh):
    in_specs = (P(None, ("feed", "freq"), None, None), P(None, None, ("feed", "freq")))
    out_specs = P("freq", None, "feed", None)
    return jax.shard_map(
        per_device, mesh=mesh, in_specs=in_specs, out_specs=out_specs, check_vma=False
    )
```

time: 607 us -> 489 us (0.81)
  waiting for transfers between devices: 417 us -> 167 us
  starting transfers between devices: 0.01 us -> 203 us
  blocking collectives: 76.7 us -> 0 us
  other arithmetic: 44.7 us -> 21.1 us
  matrix products: 35.8 us -> 57.7 us
  local copies, waits for them, and re-layouts: 18.5 us -> 39 us
  between operations: 13.4 us -> 0.36 us
    all_gather x1 -> x0, waiting for transfers between devices: 417 us -> none  [per_device(): lax.all_gather(own_rows, 'feed', axis=1, tiled=True)]
    ppermute x0 -> x16, starting transfers between devices: none -> 187 us  [the longest x4 107 us: ring_blocks(): lax.ppermute(from_right[half:], 'feed', backward)]
    ppermute x0 -> x16, waiting for transfers between devices: none -> 117 us  [the longest x4 77.4 us: ring_blocks(): from_left = lax.ppermute(from_left, 'feed', forward)]
    all_to_all x1 -> x0, blocking collectives: 76.7 us -> none  [per_device(): lax.all_to_all(blocks, 'freq', split_axis=0, concat_axis=2, tiled=True)]
    all_to_all x0 -> x4, waiting for transfers between devices: none -> 49.6 us  [per_device(): lax.all_to_all(blocks, 'freq', split_axis=0, concat_axis=0, tiled=True)]
    slice x0 -> x10, local copies, waits for them, and re-layouts: none -> 34.6 us  [the longest x1 17.9 us: per_device(): volt_imag = volts[:, channel, :, 1].astype(jnp.float32)]
    another operation x3 -> x6, other arithmetic: 41.5 us -> 9.01 us
    dot_general x1 -> x20, matrix products: 35.8 us -> 57.7 us  [correlate(): jnp.einsum('qrk,fk->qrf', stacked, columns, preferred_element_type=jnp.fl...]
  transfers between devices with their start and end apart: 1 -> 20, of which waited for: 1 -> 12; matrix products, arithmetic and copies ran while one was open for 1% -> 19% of each run, Pallas kernels for 0% -> 0%
where the time goes in v1:
time: 489 us; the launch traced here: 488 us
  starting transfers between devices  203 us (42%)
  waiting for transfers between devices  167 us (34%)
  matrix products  57.7 us (12%)
  local copies, waits for them, and re-layouts  39 us (8%)
  other arithmetic  21.1 us (4%)
    ppermute x4, starting transfers between devices, ring_blocks(): lax.ppermute(from_right[half:], 'feed', backward)  107 us
    ppermute x4, starting transfers between devices, ring_blocks(): from_right = lax.ppermute(from_right, 'feed', backward)  77.5 us
    ppermute x4, waiting for transfers between devices, ring_blocks(): from_left = lax.ppermute(from_left, 'feed', forward)  77.4 us
    dot_general x20, matrix products, correlate(): jnp.einsum('qrk,fk->qrf', stacked, columns, preferred_element_type=jnp.fl...  57.7 us
    all_to_all x4, waiting for transfers between devices, per_device(): lax.all_to_all(blocks, 'freq', split_axis=0, concat_axis=0, tiled=True)  49.6 us
    ppermute x4, waiting for transfers between devices, ring_blocks(): lax.ppermute(from_right[half:], 'feed', backward)  27.6 us
    slice x1, local copies, waits for them, and re-layouts, per_device(): volt_imag = volts[:, channel, :, 1].astype(jnp.float32)  17.9 us
    all_to_all x4, starting transfers between devices, per_device(): lax.all_to_all(blocks, 'freq', split_axis=0, concat_axis=0, tiled=True)  16.6 us
  transfers between devices with their start and end apart: 20, of which 12 were waited for; matrix products, arithmetic and copies ran while one was open for 19% of the time, Pallas kernels for 0%

profile of v1, /device:TPU:0, one launch (start us, length us, event | category | flops | bytes accessed | tf_op | source)
XLA Modules:
  0.0 488.0 jit_solution(5399585686346752361)
XLA Ops:
  0.0 17.9 %fusion.40 = (s32[8,1,64,1,768]{4,3,2,1,0:T(1,128)S(1)}, s32[8,1,64,1,768]{4,3,2,1,0:T(1,128)S(1)}, s32[8,1,64,1,768]{4,3,2,1,0:T(1,128)}, s32[8,1,64,1,768]{4,3...) fusion(s32[8,4,64,2,768]{4,3,2,1,0:T(2,128)} %bitcast.190), kind=kLoop, calls=%fused_computation.92 | loop fusion | bytes 25165824 | tf_op jit(solution)/shard_map/slice | solution.py:50
  21.3 5.2 %all-to-all-start = ((bf16[8,64,1536]{2,1,0:T(8,128)(2,1)}), bf16[8,64,1536]{2,1,0:T(8,128)(2,1)}, u32[]{:S(2)}, u32[]{:S(2)}) async-start(bf16[8,64,1536]{2,1,0:T(8,128)(2,1)} %pad_maximum_fusion.4), calls=%async_computation | async-start | bytes 3145728 | tf_op jit(solution)/shard_map/all_to_all | solution.py:56
  26.5 2.7 pad_maximum_fusion.5
  29.2 18.4 %all-to-all-done = bf16[8,64,1536]{2,1,0:T(8,128)(2,1)} async-done(((bf16[8,64,1536]{2,1,0:T(8,128)(2,1)}), bf16[8,64,1536]{2,1,0:T(8,128)(2,1)}, u32[]{:S(2)}, u32[]{:S(2)}) %all-to-all-start) | async-done | bytes 1572896 | tf_op jit(solution)/shard_map/all_to_all | solution.py:56
  47.6 4.3 all-to-all-start.1
  51.9 3.9 subtract_convert_fusion
  57.1 15.8 %all-to-all-done.1 = bf16[8,64,1536]{2,1,0:T(8,128)(2,1)} async-done(((bf16[8,64,1536]{2,1,0:T(8,128)(2,1)}), bf16[8,64,1536]{2,1,0:T(8,128)(2,1)}, u32[]{:S(2)}, u32[]{:S(2)}) %all-to-all-start.1) | async-done | bytes 1572896 | tf_op jit(solution)/shard_map/all_to_all | solution.py:56
  72.9 3.6 all-to-all-start.2
  76.5 2.1 collective-permute-start
  78.7 2.1 collective-permute-start.1
  82.1 15.4 %all-to-all-done.2 = bf16[8,64,1536]{2,1,0:T(8,128)(2,1)S(1)} async-done(((bf16[8,64,1536]{2,1,0:T(8,128)(2,1)}), bf16[8,64,1536]{2,1,0:T(8,128)(2,1)S(1)}, u32[]{:S(2)}, u32[]{:S(2)}) %all-to-all-start.2) | async-done | bytes 1572896 | tf_op jit(solution)/shard_map/all_to_all | solution.py:56
  97.5 3.6 all-to-all-start.3
  101.1 4.1 collective-permute-start.5
  108.0 2.6 fusion.43
  111.9 4.4 collective-permute-done
  116.3 35.7 %collective-permute-start.9 = (bf16[512,1536]{1,0:T(8,128)(2,1)S(1)}, bf16[512,1536]{1,0:T(8,128)(2,1)}, u32[]{:S(2)}, u32[]{:S(2)}) collective-permute-start(bf16[512,1536]{1,0:T(8,128)(2,1)S(1)} %bitcast.202), channel_id=1, source_target_pairs={{0,3},{1,0},{2,1},{3,2},{4,7},{5,4},{6,5},{7,6},{8,11},{9,8},{10,9... | collective-permute-start | bytes 4718600 | tf_op jit(solution)/shard_map/ppermute | solution.py:32
  152.0 31.8 %collective-permute-done.4 = bf16[512,1536]{1,0:T(8,128)(2,1)} collective-permute-done((bf16[512,1536]{1,0:T(8,128)(2,1)}, bf16[512,1536]{1,0:T(8,128)(2,1)}, u32[]{:S(2)}, u32[]{:S(2)}) %collective-permute-start.4) | collective-permute-done | bytes 1572896 | tf_op jit(solution)/shard_map/ppermute | solution.py:31
  183.8 35.6 %collective-permute-start.13 = (bf16[512,1536]{1,0:T(8,128)(2,1)S(1)}, bf16[512,1536]{1,0:T(8,128)(2,1)}, u32[]{:S(2)}, u32[]{:S(2)}) collective-permute-start(bf16[512,1536]{1,0:T(8,128)(2,1)S(1)} %bitcast.192), channel_id=1, source_target_pairs={{0,3},{1,0},{2,1},{3,2},{4,7},{5,4},{6,5},{7,6},{8,11},{9,8},{10,9... | collective-permute-start | bytes 4718600 | tf_op jit(solution)/shard_map/ppermute | solution.py:32
  221.6 4.1 broadcast_in_dim.63
  225.7 3.7 bitcast_dynamic-update-slice_fusion.11
  237.7 13.5 %collective-permute-done.8 = bf16[512,1536]{1,0:T(8,128)(2,1)} collective-permute-done((bf16[512,1536]{1,0:T(8,128)(2,1)S(1)}, bf16[512,1536]{1,0:T(8,128)(2,1)}, u32[]{:S(2)}, u32[]{:S(2)}) %collective-permute-start.8) | collective-permute-done | bytes 1572896 | tf_op jit(solution)/shard_map/ppermute | solution.py:31
  251.2 35.6 %collective-permute-start.3 = (bf16[256,1536]{1,0:T(8,128)(2,1)}, bf16[256,1536]{1,0:T(8,128)(2,1)}, u32[]{:S(2)}, u32[]{:S(2)}) collective-permute-start(bf16[256,1536]{1,0:T(8,128)(2,1)} %slice.135), channel_id=1, source_target_pairs={{0,3},{1,0},{2,1},{3,2},{4,7},{5,4},{6,5},{7,6},{8,11},{9,8},{10,9... | collective-permute-start | bytes 2359304 | tf_op jit(solution)/shard_map/ppermute | solution.py:29
  288.9 2.1 slice.151
  291.0 27.7 %collective-permute-done.12 = bf16[512,1536]{1,0:T(8,128)(2,1)} collective-permute-done((bf16[512,1536]{1,0:T(8,128)(2,1)S(1)}, bf16[512,1536]{1,0:T(8,128)(2,1)}, u32[]{:S(2)}, u32[]{:S(2)}) %collective-permute-start.12) | collective-permute-done | bytes 1572896 | tf_op jit(solution)/shard_map/ppermute | solution.py:31
  318.7 35.5 %collective-permute-start.7 = (bf16[256,1536]{1,0:T(8,128)(2,1)}, bf16[256,1536]{1,0:T(8,128)(2,1)}, u32[]{:S(2)}, u32[]{:S(2)}) collective-permute-start(bf16[256,1536]{1,0:T(8,128)(2,1)} %slice.143), channel_id=1, source_target_pairs={{0,3},{1,0},{2,1},{3,2},{4,7},{5,4},{6,5},{7,6},{8,11},{9,8},{10,9... | collective-permute-start | bytes 2359304 | tf_op jit(solution)/shard_map/ppermute | solution.py:29
  356.3 2.1 slice.159
  358.4 3.7 bitcast_dynamic-update-slice_fusion.10
  362.1 3.7 bitcast_dynamic-update-slice_fusion.9
  365.8 3.4 collective-permute-done.2
  369.3 18.6 %collective-permute-start.11 = (bf16[256,1536]{1,0:T(8,128)(2,1)}, bf16[256,1536]{1,0:T(8,128)(2,1)}, u32[]{:S(2)}, u32[]{:S(2)}) collective-permute-start(bf16[256,1536]{1,0:T(8,128)(2,1)} %slice.151), channel_id=1, source_target_pairs={{0,3},{1,0},{2,1},{3,2},{4,7},{5,4},{6,5},{7,6},{8,11},{9,8},{10,9... | collective-permute-start | bytes 2359304 | tf_op jit(solution)/shard_map/ppermute | solution.py:29
  387.9 2.6 fusion.31
  390.6 2.6 fusion.29
  393.2 3.7 bitcast_dynamic-update-slice_fusion.8
  396.9 3.7 bitcast_dynamic-update-slice_fusion.7
  400.7 3.8 bitcast_dynamic-update-slice_fusion.6
  404.5 17.1 %collective-permute-start.15 = (bf16[256,1536]{1,0:T(8,128)(2,1)S(1)}, bf16[256,1536]{1,0:T(8,128)(2,1)S(1)}, u32[]{:S(2)}, u32[]{:S(2)}) collective-permute-start(bf16[256,1536]{1,0:T(8,128)(2,1)S(1)} %copy-done.6), channel_id=1, source_target_pairs={{0,3},{1,0},{2,1},{3,2},{4,7},{5,4},{6,5},{7,6},{8,11},{9,8},{10,9... | collective-permute-start | bytes 2359304 | tf_op jit(solution)/shard_map/ppermute | solution.py:29
  421.6 2.6 fusion.27
  424.2 2.6 fusion.25
  428.7 3.2 bitcast_dynamic-update-slice_fusion.4
  431.9 3.2 bitcast_dynamic-update-slice_fusion.3
  436.8 2.1 fusion.23
  438.9 14.3 %collective-permute-done.11 = bf16[256,1536]{1,0:T(8,128)(2,1)} collective-permute-done((bf16[256,1536]{1,0:T(8,128)(2,1)}, bf16[256,1536]{1,0:T(8,128)(2,1)}, u32[]{:S(2)}, u32[]{:S(2)}) %collective-permute-start.11) | collective-permute-done | bytes 786464 | tf_op jit(solution)/shard_map/ppermute | solution.py:29
  453.2 2.1 fusion.21
  457.2 3.2 bitcast_dynamic-update-slice_fusion.1
  460.4 3.2 bitcast_dynamic-update-slice_fusion
  463.6 6.9 %collective-permute-done.14 = bf16[256,1536]{1,0:T(8,128)(2,1)} collective-permute-done((bf16[256,1536]{1,0:T(8,128)(2,1)}, bf16[256,1536]{1,0:T(8,128)(2,1)}, u32[]{:S(2)}, u32[]{:S(2)}) %collective-permute-start.14) | collective-permute-done | bytes 786464 | tf_op jit(solution)/shard_map/ppermute | solution.py:28
  470.5 2.1 fusion.19
  472.7 13.3 %collective-permute-done.15 = bf16[256,1536]{1,0:T(8,128)(2,1)S(1)} collective-permute-done((bf16[256,1536]{1,0:T(8,128)(2,1)S(1)}, bf16[256,1536]{1,0:T(8,128)(2,1)S(1)}, u32[]{:S(2)}, u32[]{:S(2)}) %collective-permute-start.15) | collective-permute-done | bytes 786464 | tf_op jit(solution)/shard_map/ppermute | solution.py:29
  (53 shorter events, 32.0 us)
Async XLA Ops:
  0.0 17.9 %copy-start.7 = (f32[2,32,64]{2,1,0:T(8,128)S(1)}, f32[2,32,64]{2,1,0:T(8,128)}, u32[]{:S(2)}) copy-start(f32[2,32,64]{2,1,0:T(8,128)} %param.3) | copy-start | bytes 49156
  21.3 26.3 %all-to-all-start = ((bf16[8,64,1536]{2,1,0:T(8,128)(2,1)}), bf16[8,64,1536]{2,1,0:T(8,128)(2,1)}, u32[]{:S(2)}, u32[]{:S(2)}) async-start(bf16[8,64,1536]{2,1,0:T(8,128)(2,1)} %pad_maximum_fusion.4), calls=%async_computation | async-start | bytes 3145728 | tf_op jit(solution)/shard_map/all_to_all | solution.py:56
  47.6 25.3 %all-to-all-start.1 = ((bf16[8,64,1536]{2,1,0:T(8,128)(2,1)}), bf16[8,64,1536]{2,1,0:T(8,128)(2,1)}, u32[]{:S(2)}, u32[]{:S(2)}) async-start(bf16[8,64,1536]{2,1,0:T(8,128)(2,1)} %pad_maximum_fusion.5), calls=%async_computation.1 | async-start | bytes 3145728 | tf_op jit(solution)/shard_map/all_to_all | solution.py:56
  57.1 23.7 %copy-start.1 = (bf16[8,64,768]{2,1,0:T(8,128)(2,1)S(1)}, bf16[8,64,768]{2,1,0:T(8,128)(2,1)}, u32[]{:S(2)}) copy-start(bf16[8,64,768]{2,1,0:T(8,128)(2,1)} %get-tuple-element.13) | copy-start | bytes 2359300
  57.1 23.7 %copy-start.2 = (bf16[8,64,768]{2,1,0:T(8,128)(2,1)S(1)}, bf16[8,64,768]{2,1,0:T(8,128)(2,1)}, u32[]{:S(2)}) copy-start(bf16[8,64,768]{2,1,0:T(8,128)(2,1)} %get-tuple-element.14) | copy-start | bytes 2359300
  72.9 24.5 %all-to-all-start.2 = ((bf16[8,64,1536]{2,1,0:T(8,128)(2,1)}), bf16[8,64,1536]{2,1,0:T(8,128)(2,1)S(1)}, u32[]{:S(2)}, u32[]{:S(2)}) async-start(bf16[8,64,1536]{2,1,0:T(8,128)(2,1)} %pad_maximum_fusion.6), calls=%async_computation.2 | async-start | bytes 3145728 | tf_op jit(solution)/shard_map/all_to_all | solution.py:56
  76.5 39.8 %collective-permute-start = (bf16[512,1536]{1,0:T(8,128)(2,1)}, bf16[512,1536]{1,0:T(8,128)(2,1)}, u32[]{:S(2)}, u32[]{:S(2)}) collective-permute-start(bf16[512,1536]{1,0:T(8,128)(2,1)} %bitcast.7), channel_id=1, source_target_pairs={{0,1},{1,2},{2,3},{3,0},{4,5},{5,6},{6,7},{7,4},{8,9},{9,10},{10,1... | collective-permute-start | bytes 4718600 | tf_op jit(solution)/shard_map/ppermute | solution.py:31
  78.7 73.3 %collective-permute-start.1 = (bf16[512,1536]{1,0:T(8,128)(2,1)}, bf16[512,1536]{1,0:T(8,128)(2,1)}, u32[]{:S(2)}, u32[]{:S(2)}) collective-permute-start(bf16[512,1536]{1,0:T(8,128)(2,1)} %bitcast.7), channel_id=1, source_target_pairs={{0,3},{1,0},{2,1},{3,2},{4,7},{5,4},{6,5},{7,6},{8,11},{9,8},{10,9... | collective-permute-start | bytes 4718600 | tf_op jit(solution)/shard_map/ppermute | solution.py:32
  80.8 103.0 %collective-permute-start.4 = (bf16[512,1536]{1,0:T(8,128)(2,1)}, bf16[512,1536]{1,0:T(8,128)(2,1)}, u32[]{:S(2)}, u32[]{:S(2)}) collective-permute-start(bf16[512,1536]{1,0:T(8,128)(2,1)} %bitcast.24), channel_id=1, source_target_pairs={{0,1},{1,2},{2,3},{3,0},{4,5},{5,6},{6,7},{7,4},{8,9},{9,10},{10,1... | collective-permute-start | bytes 4718600 | tf_op jit(solution)/shard_map/ppermute | solution.py:31
  97.5 54.5 %all-to-all-start.3 = ((bf16[8,64,1536]{2,1,0:T(8,128)(2,1)}), bf16[8,64,1536]{2,1,0:T(8,128)(2,1)S(1)}, u32[]{:S(2)}, u32[]{:S(2)}) async-start(bf16[8,64,1536]{2,1,0:T(8,128)(2,1)} %pad_maximum_fusion.7), calls=%async_computation.3 | async-start | bytes 3145728 | tf_op jit(solution)/shard_map/all_to_all | solution.py:56
  101.1 134.5 %collective-permute-start.5 = (bf16[512,1536]{1,0:T(8,128)(2,1)}, bf16[512,1536]{1,0:T(8,128)(2,1)}, u32[]{:S(2)}, u32[]{:S(2)}) collective-permute-start(bf16[512,1536]{1,0:T(8,128)(2,1)} %bitcast.24), channel_id=1, source_target_pairs={{0,3},{1,0},{2,1},{3,2},{4,7},{5,4},{6,5},{7,6},{8,11},{9,8},{10,9... | collective-permute-start | bytes 4718600 | tf_op jit(solution)/shard_map/ppermute | solution.py:32
  105.2 146.0 %collective-permute-start.8 = (bf16[512,1536]{1,0:T(8,128)(2,1)S(1)}, bf16[512,1536]{1,0:T(8,128)(2,1)}, u32[]{:S(2)}, u32[]{:S(2)}) collective-permute-start(bf16[512,1536]{1,0:T(8,128)(2,1)S(1)} %bitcast.200), channel_id=1, source_target_pairs={{0,1},{1,2},{2,3},{3,0},{4,5},{5,6},{6,7},{7,4},{8,9},{9,10},{10,1... | collective-permute-start | bytes 4718600 | tf_op jit(solution)/shard_map/ppermute | solution.py:31
  116.3 172.6 %collective-permute-start.9 = (bf16[512,1536]{1,0:T(8,128)(2,1)S(1)}, bf16[512,1536]{1,0:T(8,128)(2,1)}, u32[]{:S(2)}, u32[]{:S(2)}) collective-permute-start(bf16[512,1536]{1,0:T(8,128)(2,1)S(1)} %bitcast.202), channel_id=1, source_target_pairs={{0,3},{1,0},{2,1},{3,2},{4,7},{5,4},{6,5},{7,6},{8,11},{9,8},{10,9... | collective-permute-start | bytes 4718600 | tf_op jit(solution)/shard_map/ppermute | solution.py:32
  152.0 166.7 %collective-permute-start.12 = (bf16[512,1536]{1,0:T(8,128)(2,1)S(1)}, bf16[512,1536]{1,0:T(8,128)(2,1)}, u32[]{:S(2)}, u32[]{:S(2)}) collective-permute-start(bf16[512,1536]{1,0:T(8,128)(2,1)S(1)} %bitcast.191), channel_id=1, source_target_pairs={{0,1},{1,2},{2,3},{3,0},{4,5},{5,6},{6,7},{7,4},{8,9},{9,10},{10,1... | collective-permute-start | bytes 4718600 | tf_op jit(solution)/shard_map/ppermute | solution.py:31
  183.8 172.5 %collective-permute-start.13 = (bf16[512,1536]{1,0:T(8,128)(2,1)S(1)}, bf16[512,1536]{1,0:T(8,128)(2,1)}, u32[]{:S(2)}, u32[]{:S(2)}) collective-permute-start(bf16[512,1536]{1,0:T(8,128)(2,1)S(1)} %bitcast.192), channel_id=1, source_target_pairs={{0,3},{1,0},{2,1},{3,2},{4,7},{5,4},{6,5},{7,6},{8,11},{9,8},{10,9... | collective-permute-start | bytes 4718600 | tf_op jit(solution)/shard_map/ppermute | solution.py:32
  219.4 1.6 copy-start.3
  219.4 1.8 copy-start.4
  221.6 4.1 copy-start.5
  235.6 133.6 %collective-permute-start.2 = (bf16[256,1536]{1,0:T(8,128)(2,1)}, bf16[256,1536]{1,0:T(8,128)(2,1)}, u32[]{:S(2)}, u32[]{:S(2)}) collective-permute-start(bf16[256,1536]{1,0:T(8,128)(2,1)} %slice.134), channel_id=1, source_target_pairs={{0,1},{1,2},{2,3},{3,0},{4,5},{5,6},{6,7},{7,4},{8,9},{9,10},{10,1... | collective-permute-start | bytes 2359304 | tf_op jit(solution)/shard_map/ppermute | solution.py:28
  251.2 139.3 %collective-permute-start.3 = (bf16[256,1536]{1,0:T(8,128)(2,1)}, bf16[256,1536]{1,0:T(8,128)(2,1)}, u32[]{:S(2)}, u32[]{:S(2)}) collective-permute-start(bf16[256,1536]{1,0:T(8,128)(2,1)} %slice.135), channel_id=1, source_target_pairs={{0,3},{1,0},{2,1},{3,2},{4,7},{5,4},{6,5},{7,6},{8,11},{9,8},{10,9... | collective-permute-start | bytes 2359304 | tf_op jit(solution)/shard_map/ppermute | solution.py:29
  288.9 115.6 %collective-permute-start.6 = (bf16[256,1536]{1,0:T(8,128)(2,1)}, bf16[256,1536]{1,0:T(8,128)(2,1)}, u32[]{:S(2)}, u32[]{:S(2)}) collective-permute-start(bf16[256,1536]{1,0:T(8,128)(2,1)} %slice.142), channel_id=1, source_target_pairs={{0,1},{1,2},{2,3},{3,0},{4,5},{5,6},{6,7},{7,4},{8,9},{9,10},{10,1... | collective-permute-start | bytes 2359304 | tf_op jit(solution)/shard_map/ppermute | solution.py:28
  318.7 105.5 %collective-permute-start.7 = (bf16[256,1536]{1,0:T(8,128)(2,1)}, bf16[256,1536]{1,0:T(8,128)(2,1)}, u32[]{:S(2)}, u32[]{:S(2)}) collective-permute-start(bf16[256,1536]{1,0:T(8,128)(2,1)} %slice.143), channel_id=1, source_target_pairs={{0,3},{1,0},{2,1},{3,2},{4,7},{5,4},{6,5},{7,6},{8,11},{9,8},{10,9... | collective-permute-start | bytes 2359304 | tf_op jit(solution)/shard_map/ppermute | solution.py:29
  356.3 80.5 %collective-permute-start.10 = (bf16[256,1536]{1,0:T(8,128)(2,1)}, bf16[256,1536]{1,0:T(8,128)(2,1)}, u32[]{:S(2)}, u32[]{:S(2)}) collective-permute-start(bf16[256,1536]{1,0:T(8,128)(2,1)} %slice.150), channel_id=1, source_target_pairs={{0,1},{1,2},{2,3},{3,0},{4,5},{5,6},{6,7},{7,4},{8,9},{9,10},{10,1... | collective-permute-start | bytes 2359304 | tf_op jit(solution)/shard_map/ppermute | solution.py:28
  369.3 83.9 %collective-permute-start.11 = (bf16[256,1536]{1,0:T(8,128)(2,1)}, bf16[256,1536]{1,0:T(8,128)(2,1)}, u32[]{:S(2)}, u32[]{:S(2)}) collective-permute-start(bf16[256,1536]{1,0:T(8,128)(2,1)} %slice.151), channel_id=1, source_target_pairs={{0,3},{1,0},{2,1},{3,2},{4,7},{5,4},{6,5},{7,6},{8,11},{9,8},{10,9... | collective-permute-start | bytes 2359304 | tf_op jit(solution)/shard_map/ppermute | solution.py:29
  390.5 80.0 %collective-permute-start.14 = (bf16[256,1536]{1,0:T(8,128)(2,1)}, bf16[256,1536]{1,0:T(8,128)(2,1)}, u32[]{:S(2)}, u32[]{:S(2)}) collective-permute-start(bf16[256,1536]{1,0:T(8,128)(2,1)} %slice.158), channel_id=1, source_target_pairs={{0,1},{1,2},{2,3},{3,0},{4,5},{5,6},{6,7},{7,4},{8,9},{9,10},{10,1... | collective-permute-start | bytes 2359304 | tf_op jit(solution)/shard_map/ppermute | solution.py:28
  400.7 3.8 copy-start.6
  404.5 81.5 %collective-permute-start.15 = (bf16[256,1536]{1,0:T(8,128)(2,1)S(1)}, bf16[256,1536]{1,0:T(8,128)(2,1)S(1)}, u32[]{:S(2)}, u32[]{:S(2)}) collective-permute-start(bf16[256,1536]{1,0:T(8,128)(2,1)S(1)} %copy-done.6), channel_id=1, source_target_pairs={{0,3},{1,0},{2,1},{3,2},{4,7},{5,4},{6,5},{7,6},{8,11},{9,8},{10,9... | collective-permute-start | bytes 2359304 | tf_op jit(solution)/shard_map/ppermute | solution.py:29
  472.7 13.3 %copy-start = (f32[4,2,512,2048]{3,2,1,0:T(8,128)}, f32[4,2,512,2048]{3,2,1,0:T(8,128)S(1)}, u32[]{:S(2)}) copy-start(f32[4,2,512,2048]{3,2,1,0:T(8,128)S(1)} %fusion.19) | copy-start | bytes 100663296
